TPU v7x, 32 devices: a whole 2x2x4 slice. The times are simulated.
32 devices in a mesh: row: 4 (over z), col: 8 (over y, x, core).
Axes of the slice: x: 2, y: 2, z: 4, core: 2. Of those that a mesh axis runs over, the one named last changes fastest.
Arguments:
- build_key: int32 [8, 8, 128], P('col', 'row'), may hold values from -1 to 63, as said below
- build_part: int32 [8, 8], P('col', 'row'), may hold values from 0 to 1023, as said below
- build_payload: float32 [8, 8, 128, 128], P('col', 'row'), may hold values from -6 to 6
- probe_key: int32 [4, 8, 8, 8, 128], P('row', 'col'), may hold values from -2 to 63, as said below
- probe_part: int32 [4, 8, 8, 8, 128], P('row', 'col'), may hold values from 0 to 1023, as said below
Outputs:
- joined: float32 [4, 8, 8, 8, 128, 128], P('row', 'col')
- match_position: float32 [4, 8, 8, 8, 128], P('row', 'col')
- match_rate: float32 [1024], replicated
Inputs may be any that keep to these rules, and one draw needn't show every extreme that they name: Each column c owns a set of 128 partitions, disjoint from the other columns' sets; build_part[c, t] lies in column c's set. `build_key`: -1 marks padding rows, which lie at the end of a tile. `probe_key`: -2 marks padding rows, which lie at the end of a tile. probe_part[r, s, c, q, i] lies in the set of partitions owned by column c.
All inputs are finite; a program needn't handle non-finite values.
Results may differ from a plain program's by a relative error of at most 0.0003.
Values sent between devices are 32-bit elements; how exact they have to be, the bound alone decides.
A program may use at most 256 MiB of HBM per device.

v0:
```python
import jax
import jax.numpy as jnp
from jax import lax
from jax.sharding import PartitionSpec as P

PARTS_SIZE = 1024


def tile_join(probe_keys, probe_parts, build_keys, build_parts, payload, positions):
    count_tiles = build_keys.shape[0]
    tile_rows = build_keys.shape[1]
    flat_keys = build_keys.reshape(-1)
    flat_parts = jnp.broadcast_to(build_parts.reshape(-1, 1), (count_tiles, tile_rows)).reshape(-1)
    flat_payload = payload.reshape(count_tiles * tile_rows, payload.shape[-1])
    side_columns = jnp.stack([positions, jnp.ones_like(positions)], axis=1)

    def tile_one_block(block_args):
        block_keys, block_parts = block_args
        matched = (
            (block_keys[:, None] == flat_keys[None, :])
            & (block_parts[:, None] == flat_parts[None, :])
        ).astype(jnp.float32)
        summed = jnp.dot(
            matched,
            flat_payload,
            precision=lax.Precision.HIGHEST,
            preferred_element_type=jnp.float32,
        )
        sidebar = jnp.dot(
            matched,
            side_columns,
            precision=lax.Precision.HIGHEST,
            preferred_element_type=jnp.float32,
        )
        return (summed, sidebar[:, 0], sidebar[:, 1])

    return lax.map(tile_one_block, (probe_keys, probe_parts))


def place_rows(tile_count, tile_rows, whole_rows):
    offsets = jnp.arange(tile_count * tile_rows, dtype=jnp.int32)
    return offsets.astype(jnp.float32) / float(whole_rows)


def add_pieces(probe_keys, probe_parts, pieces, positions):
    piece_keys, piece_parts, piece_payload = pieces
    summed, placed, counted = tile_join(
        probe_keys, probe_parts, piece_keys[0], piece_parts[0], piece_payload[0], positions
    )
    return (summed, placed, counted)


def partition_sums(part_ids, values, blocks):
    block_ids = part_ids.reshape(blocks, -1)
    block_values = values.reshape(blocks, block_ids.shape[1], values.shape[-1])
    labels = jnp.arange(PARTS_SIZE, dtype=jnp.int32)

    def partition_one_block(block_args):
        ids_here, values_here = block_args
        onehot = (labels[:, None] == ids_here[None, :]).astype(jnp.float32)
        return jnp.dot(
            onehot, values_here, precision=lax.Precision.HIGHEST, preferred_element_type=jnp.float32
        )

    return jnp.sum(lax.map(partition_one_block, (block_ids, block_values)), axis=0)


def local(build_key, build_part, build_payload, probe_key, probe_part):
    build_keys = build_key.astype(jnp.float32)
    build_parts = build_part.astype(jnp.float32)
    columns = build_payload.shape[-1]
    tile_rows = build_key.shape[-1]
    local_tiles = build_key.shape[1]
    whole_rows = local_tiles * lax.axis_size("row") * tile_rows
    owners = probe_key.shape[2]
    probe_tiles = probe_key.shape[3]
    got_keys, got_parts = (
        lax.all_to_all(probe_key, "col", split_axis=2, concat_axis=1, tiled=True),
        lax.all_to_all(probe_part, "col", split_axis=2, concat_axis=1, tiled=True),
    )
    probe_keys = got_keys.reshape(owners, probe_tiles * tile_rows).astype(jnp.float32)
    probe_parts = got_parts.reshape(owners, probe_tiles * tile_rows).astype(jnp.float32)
    pieces = (
        lax.all_gather(build_keys, "row", axis=1, tiled=True),
        lax.all_gather(build_parts, "row", axis=1, tiled=True),
        lax.all_gather(build_payload, "row", axis=1, tiled=True),
    )
    positions = place_rows(pieces[0].shape[1], tile_rows, whole_rows)
    summed, placed, counted = add_pieces(probe_keys, probe_parts, pieces, positions)
    joined = summed.reshape(1, owners, 1, probe_tiles, tile_rows, columns)
    places = placed.reshape(1, owners, 1, probe_tiles, tile_rows)
    counts = counted.reshape(1, owners, 1, probe_tiles, tile_rows)
    back_joined, back_places, back_counts = (
        lax.all_to_all(joined, "col", split_axis=1, concat_axis=2, tiled=True),
        lax.all_to_all(places, "col", split_axis=1, concat_axis=2, tiled=True),
        lax.all_to_all(counts, "col", split_axis=1, concat_axis=2, tiled=True),
    )
    part_ids = probe_part.reshape(-1)
    live_rows = (probe_key >= 0).astype(jnp.float32).reshape(-1)
    both_columns = jnp.stack([back_counts.reshape(-1), live_rows], axis=1)
    local_sums = partition_sums(part_ids, both_columns, owners)
    match_total, live_total = lax.psum((local_sums[:, 0], local_sums[:, 1]), ("row", "col"))
    return (back_joined, back_places, match_total / jnp.maximum(live_total, 1.0))


def solution(mesh):
    return jax.shard_map(
        local,
        mesh=mesh,
        in_specs=(
            P("col", "row", None),
            P("col", "row"),
            P("col", "row", None, None),
            P("row", "col", None, None, None),
            P("row", "col", None, None, None),
        ),
        out_specs=(P("row", "col", None, None, None, None), P("row", "col", None, None, None), P()),
        check_vma=False,
    )
```

profile of v0, /device:TPU:0, one launch (start us, length us, event | category | flops | bytes accessed | tf_op | source)
XLA Modules:
  0.0 205.3 jit_solution(17796106191170032106)
XLA Ops:
  0.6 5.2 %all-to-all-start.1 = ((s32[1,1,8,8,128]{4,3,1,0,2:T(8,128)}), s32[1,1,8,8,128]{4,3,1,0,2:T(8,128)S(1)}, u32[]{:S(2)}, u32[]{:S(2)}) async-start(s32[1,1,8,8,128]{4,3,1,0,2:T(8,128)} %bitcast.95), calls=%async_computation.1 | async-start | bytes 65536 | tf_op jit(solution)/shard_map/all_to_all | solution.py:79
  5.8 16.7 %all_gather.11 = f32[1,8,128,128]{3,2,0,1:T(8,128)S(1)} all-gather(f32[1,2,128,128]{3,2,0,1:T(8,128)} %bitcast.94), channel_id=1, replica_groups=mesh['row'=4,'col'=8] {'row'}, dimensions={1}, use_global_device_ids=true | all-gather | bytes 655360 | tf_op jit(solution)/shard_map/all_gather | solution.py:86
  22.5 1.2 dynamic-slice
  24.4 0.8 bitcast_dynamic-update-slice_fusion
  25.2 11.9 %all-reduce.1 = f32[8]{0:T(128)S(1)} all-reduce(f32[8]{0:T(128)S(1)} %bitcast_dynamic-update-slice_fusion), channel_id=1, replica_groups=mesh['row'=4,'col'=8] {'row'}, use_global_device_ids=true, to_apply=%add.1 | all-reduce | flops 8 | bytes 64
  37.1 0.7 convert_element_type.33
  37.8 7.6 %all_gather.9 = f32[1,8,128]{2,0,1:T(1,128)S(1)} all-gather(f32[1,2,128]{2,0,1:T(1,128)S(1)} %bitcast.117), channel_id=1, replica_groups=mesh['row'=4,'col'=8] {'row'}, dimensions={1}, use_global_device_ids=true | all-gather | bytes 5120 | tf_op jit(solution)/shard_map/all_gather | solution.py:84
  45.4 4.2 %all-to-all-start = ((s32[1,1,8,8,128]{4,3,1,0,2:T(8,128)}), s32[1,1,8,8,128]{4,3,1,0,2:T(8,128)S(1)}, u32[]{:S(2)}, u32[]{:S(2)}) async-start(s32[1,1,8,8,128]{4,3,1,0,2:T(8,128)} %bitcast.97), calls=%async_computation | async-start | bytes 65536 | tf_op jit(solution)/shard_map/all_to_all | solution.py:78
  49.6 4.8 %all-to-all-done = s32[1,1,8,8,128]{4,3,1,0,2:T(8,128)S(1)} async-done(((s32[1,1,8,8,128]{4,3,1,0,2:T(8,128)}), s32[1,1,8,8,128]{4,3,1,0,2:T(8,128)S(1)}, u32[]{:S(2)}, u32[]{:S(2)}) %all-to-all-start) | async-done | bytes 32800 | tf_op jit(solution)/shard_map/all_to_all | solution.py:78
  54.4 43.4 %while.26 = (s32[]{:T(128)}, f32[8,1024,128]{2,1,0:T(8,128)}, f32[8,1024]{1,0:T(8,128)S(1)}, f32[8,1024]{1,0:T(8,128)S(1)}, f32[8,1024]{1,0:T(8,128)S(1)}, /*ind...) while((s32[]{:T(128)}, f32[8,1024,128]{2,1,0:T(8,128)}, ...), condition=%wide.region_1.2_spmd.clone, body=%wide.region_0.1_spmd.clone.sunk | while | flops 1642070016 | bytes 1151649 | solution.py:37
  54.4 0.1 broadcast_bitcast_fusion.2
  54.5 2.1 %fusion.35 = f32[1024,2]{0,1:T(2,128)S(1)} fusion(f32[1024,2]{0,1:T(2,128)S(1)} %get-tuple-element.303, f32[1024]{0:T(1024)S(1)} %broadcast_bitcast_fusion.2, f32[1024]{0:T(1024)S(1)} %bitcast.115, f32[1024]{0:T(1024)S(1)} %bitcast.103, f32[1024]{0:T(1024)S(1)} %bitcast.105), kind=kOutput, calls=%fused_computation.3.clone.1 | convolution fusion | flops 28311552 | bytes 32768 | tf_op jit(solution)/shard_map/while/body/eval_jaxpr/dot_general | solution.py:29
  56.7 0.1 dynamic_update_slice.26
  56.8 0.1 dynamic_update_slice.27
  56.9 2.9 %fusion.34 = f32[8,1024,128]{2,1,0:T(8,128)} fusion(f32[8,1024,128]{2,1,0:T(8,128)} %get-tuple-element.284, s32[]{:T(128)} %get-tuple-element.283, f32[1024,128]{1,0:T(8,128)S(1)} %get-tuple-element.302, f32[1024]{0:T(1024)S(1)} %broadcast_bitcast_fusion.2, f32[1024]{0:T(1024)S(1)} %bitcast.116, f32[1024]{0:T(1024)S(1)} %bitcast.104, ...), kind=kOutput, calls=%fused_computation.14.clone.1 | convolution fusion | flops 1613758464 | bytes 1065472 | tf_op jit(solution)/shard_map/while/body/eval_jaxpr/dot_general | solution.py:23
  59.9 0.1 broadcast_bitcast_fusion.2
  59.9 2.1 %fusion.35 = f32[1024,2]{0,1:T(2,128)S(1)} fusion(f32[1024,2]{0,1:T(2,128)S(1)} %get-tuple-element.303, f32[1024]{0:T(1024)S(1)} %broadcast_bitcast_fusion.2, f32[1024]{0:T(1024)S(1)} %bitcast.115, f32[1024]{0:T(1024)S(1)} %bitcast.103, f32[1024]{0:T(1024)S(1)} %bitcast.105), kind=kOutput, calls=%fused_computation.3.clone.1 | convolution fusion | flops 28311552 | bytes 32768 | tf_op jit(solution)/shard_map/while/body/eval_jaxpr/dot_general | solution.py:29
  62.1 0.1 dynamic_update_slice.26
  62.2 0.1 dynamic_update_slice.27
  62.3 2.9 %fusion.34 = f32[8,1024,128]{2,1,0:T(8,128)} fusion(f32[8,1024,128]{2,1,0:T(8,128)} %get-tuple-element.284, s32[]{:T(128)} %get-tuple-element.283, f32[1024,128]{1,0:T(8,128)S(1)} %get-tuple-element.302, f32[1024]{0:T(1024)S(1)} %broadcast_bitcast_fusion.2, f32[1024]{0:T(1024)S(1)} %bitcast.116, f32[1024]{0:T(1024)S(1)} %bitcast.104, ...), kind=kOutput, calls=%fused_computation.14.clone.1 | convolution fusion | flops 1613758464 | bytes 1065472 | tf_op jit(solution)/shard_map/while/body/eval_jaxpr/dot_general | solution.py:23
  65.3 0.1 broadcast_bitcast_fusion.2
  65.4 2.1 %fusion.35 = f32[1024,2]{0,1:T(2,128)S(1)} fusion(f32[1024,2]{0,1:T(2,128)S(1)} %get-tuple-element.303, f32[1024]{0:T(1024)S(1)} %broadcast_bitcast_fusion.2, f32[1024]{0:T(1024)S(1)} %bitcast.115, f32[1024]{0:T(1024)S(1)} %bitcast.103, f32[1024]{0:T(1024)S(1)} %bitcast.105), kind=kOutput, calls=%fused_computation.3.clone.1 | convolution fusion | flops 28311552 | bytes 32768 | tf_op jit(solution)/shard_map/while/body/eval_jaxpr/dot_general | solution.py:29
  67.5 0.1 dynamic_update_slice.26
  67.7 0.1 dynamic_update_slice.27
  67.8 2.9 %fusion.34 = f32[8,1024,128]{2,1,0:T(8,128)} fusion(f32[8,1024,128]{2,1,0:T(8,128)} %get-tuple-element.284, s32[]{:T(128)} %get-tuple-element.283, f32[1024,128]{1,0:T(8,128)S(1)} %get-tuple-element.302, f32[1024]{0:T(1024)S(1)} %broadcast_bitcast_fusion.2, f32[1024]{0:T(1024)S(1)} %bitcast.116, f32[1024]{0:T(1024)S(1)} %bitcast.104, ...), kind=kOutput, calls=%fused_computation.14.clone.1 | convolution fusion | flops 1613758464 | bytes 1065472 | tf_op jit(solution)/shard_map/while/body/eval_jaxpr/dot_general | solution.py:23
  70.7 0.1 broadcast_bitcast_fusion.2
  70.8 2.1 %fusion.35 = f32[1024,2]{0,1:T(2,128)S(1)} fusion(f32[1024,2]{0,1:T(2,128)S(1)} %get-tuple-element.303, f32[1024]{0:T(1024)S(1)} %broadcast_bitcast_fusion.2, f32[1024]{0:T(1024)S(1)} %bitcast.115, f32[1024]{0:T(1024)S(1)} %bitcast.103, f32[1024]{0:T(1024)S(1)} %bitcast.105), kind=kOutput, calls=%fused_computation.3.clone.1 | convolution fusion | flops 28311552 | bytes 32768 | tf_op jit(solution)/shard_map/while/body/eval_jaxpr/dot_general | solution.py:29
  73.0 0.1 dynamic_update_slice.26
  73.1 0.1 dynamic_update_slice.27
  73.2 2.9 %fusion.34 = f32[8,1024,128]{2,1,0:T(8,128)} fusion(f32[8,1024,128]{2,1,0:T(8,128)} %get-tuple-element.284, s32[]{:T(128)} %get-tuple-element.283, f32[1024,128]{1,0:T(8,128)S(1)} %get-tuple-element.302, f32[1024]{0:T(1024)S(1)} %broadcast_bitcast_fusion.2, f32[1024]{0:T(1024)S(1)} %bitcast.116, f32[1024]{0:T(1024)S(1)} %bitcast.104, ...), kind=kOutput, calls=%fused_computation.14.clone.1 | convolution fusion | flops 1613758464 | bytes 1065472 | tf_op jit(solution)/shard_map/while/body/eval_jaxpr/dot_general | solution.py:23
  76.2 2.1 %fusion.35 = f32[1024,2]{0,1:T(2,128)S(1)} fusion(f32[1024,2]{0,1:T(2,128)S(1)} %get-tuple-element.303, f32[1024]{0:T(1024)S(1)} %broadcast_bitcast_fusion.2, f32[1024]{0:T(1024)S(1)} %bitcast.115, f32[1024]{0:T(1024)S(1)} %bitcast.103, f32[1024]{0:T(1024)S(1)} %bitcast.105), kind=kOutput, calls=%fused_computation.3.clone.1 | convolution fusion | flops 28311552 | bytes 32768 | tf_op jit(solution)/shard_map/while/body/eval_jaxpr/dot_general | solution.py:29
  78.4 0.1 dynamic_update_slice.26
  78.5 0.1 dynamic_update_slice.27
  78.6 2.9 %fusion.34 = f32[8,1024,128]{2,1,0:T(8,128)} fusion(f32[8,1024,128]{2,1,0:T(8,128)} %get-tuple-element.284, s32[]{:T(128)} %get-tuple-element.283, f32[1024,128]{1,0:T(8,128)S(1)} %get-tuple-element.302, f32[1024]{0:T(1024)S(1)} %broadcast_bitcast_fusion.2, f32[1024]{0:T(1024)S(1)} %bitcast.116, f32[1024]{0:T(1024)S(1)} %bitcast.104, ...), kind=kOutput, calls=%fused_computation.14.clone.1 | convolution fusion | flops 1613758464 | bytes 1065472 | tf_op jit(solution)/shard_map/while/body/eval_jaxpr/dot_general | solution.py:23
  81.6 2.1 %fusion.35 = f32[1024,2]{0,1:T(2,128)S(1)} fusion(f32[1024,2]{0,1:T(2,128)S(1)} %get-tuple-element.303, f32[1024]{0:T(1024)S(1)} %broadcast_bitcast_fusion.2, f32[1024]{0:T(1024)S(1)} %bitcast.115, f32[1024]{0:T(1024)S(1)} %bitcast.103, f32[1024]{0:T(1024)S(1)} %bitcast.105), kind=kOutput, calls=%fused_computation.3.clone.1 | convolution fusion | flops 28311552 | bytes 32768 | tf_op jit(solution)/shard_map/while/body/eval_jaxpr/dot_general | solution.py:29
  83.8 0.1 dynamic_update_slice.26
  83.9 0.1 dynamic_update_slice.27
  84.0 2.9 %fusion.34 = f32[8,1024,128]{2,1,0:T(8,128)} fusion(f32[8,1024,128]{2,1,0:T(8,128)} %get-tuple-element.284, s32[]{:T(128)} %get-tuple-element.283, f32[1024,128]{1,0:T(8,128)S(1)} %get-tuple-element.302, f32[1024]{0:T(1024)S(1)} %broadcast_bitcast_fusion.2, f32[1024]{0:T(1024)S(1)} %bitcast.116, f32[1024]{0:T(1024)S(1)} %bitcast.104, ...), kind=kOutput, calls=%fused_computation.14.clone.1 | convolution fusion | flops 1613758464 | bytes 1065472 | tf_op jit(solution)/shard_map/while/body/eval_jaxpr/dot_general | solution.py:23
  87.1 2.1 %fusion.35 = f32[1024,2]{0,1:T(2,128)S(1)} fusion(f32[1024,2]{0,1:T(2,128)S(1)} %get-tuple-element.303, f32[1024]{0:T(1024)S(1)} %broadcast_bitcast_fusion.2, f32[1024]{0:T(1024)S(1)} %bitcast.115, f32[1024]{0:T(1024)S(1)} %bitcast.103, f32[1024]{0:T(1024)S(1)} %bitcast.105), kind=kOutput, calls=%fused_computation.3.clone.1 | convolution fusion | flops 28311552 | bytes 32768 | tf_op jit(solution)/shard_map/while/body/eval_jaxpr/dot_general | solution.py:29
  89.2 0.1 dynamic_update_slice.26
  89.4 0.1 dynamic_update_slice.27
  89.5 2.9 %fusion.34 = f32[8,1024,128]{2,1,0:T(8,128)} fusion(f32[8,1024,128]{2,1,0:T(8,128)} %get-tuple-element.284, s32[]{:T(128)} %get-tuple-element.283, f32[1024,128]{1,0:T(8,128)S(1)} %get-tuple-element.302, f32[1024]{0:T(1024)S(1)} %broadcast_bitcast_fusion.2, f32[1024]{0:T(1024)S(1)} %bitcast.116, f32[1024]{0:T(1024)S(1)} %bitcast.104, ...), kind=kOutput, calls=%fused_computation.14.clone.1 | convolution fusion | flops 1613758464 | bytes 1065472 | tf_op jit(solution)/shard_map/while/body/eval_jaxpr/dot_general | solution.py:23
  92.5 2.1 %fusion.35 = f32[1024,2]{0,1:T(2,128)S(1)} fusion(f32[1024,2]{0,1:T(2,128)S(1)} %get-tuple-element.303, f32[1024]{0:T(1024)S(1)} %broadcast_bitcast_fusion.2, f32[1024]{0:T(1024)S(1)} %bitcast.115, f32[1024]{0:T(1024)S(1)} %bitcast.103, f32[1024]{0:T(1024)S(1)} %bitcast.105), kind=kOutput, calls=%fused_computation.3.clone.1 | convolution fusion | flops 28311552 | bytes 32768 | tf_op jit(solution)/shard_map/while/body/eval_jaxpr/dot_general | solution.py:29
  94.7 0.1 dynamic_update_slice.26
  94.8 0.1 dynamic_update_slice.27
  94.9 2.9 %fusion.34 = f32[8,1024,128]{2,1,0:T(8,128)} fusion(f32[8,1024,128]{2,1,0:T(8,128)} %get-tuple-element.284, s32[]{:T(128)} %get-tuple-element.283, f32[1024,128]{1,0:T(8,128)S(1)} %get-tuple-element.302, f32[1024]{0:T(1024)S(1)} %broadcast_bitcast_fusion.2, f32[1024]{0:T(1024)S(1)} %bitcast.116, f32[1024]{0:T(1024)S(1)} %bitcast.104, ...), kind=kOutput, calls=%fused_computation.14.clone.1 | convolution fusion | flops 1613758464 | bytes 1065472 | tf_op jit(solution)/shard_map/while/body/eval_jaxpr/dot_general | solution.py:23
  97.8 0.6 copy.32
  98.5 3.3 %all-to-all-start.4 = ((f32[1,8,1,8,128]{4,3,2,0,1:T(8,128)}), f32[1,8,1,8,128]{4,3,2,0,1:T(8,128)S(1)}, u32[]{:S(2)}, u32[]{:S(2)}) async-start(f32[1,8,1,8,128]{4,3,2,0,1:T(8,128)} %bitcast.65), calls=%async_computation.4 | async-start | bytes 65536 | tf_op jit(solution)/shard_map/all_to_all | solution.py:96
  101.8 4.8 %all-to-all-done.4 = f32[1,8,1,8,128]{4,3,2,0,1:T(8,128)S(1)} async-done(((f32[1,8,1,8,128]{4,3,2,0,1:T(8,128)}), f32[1,8,1,8,128]{4,3,2,0,1:T(8,128)S(1)}, u32[]{:S(2)}, u32[]{:S(2)}) %all-to-all-start.4) | async-done | bytes 32800 | tf_op jit(solution)/shard_map/all_to_all | solution.py:96
  106.6 7.2 %all_to_all.51 = f32[1,8,1,8,128]{4,3,2,0,1:T(8,128)S(1)} all-to-all(f32[1,8,1,8,128]{4,3,2,0,1:T(8,128)S(1)} %bitcast.99), channel_id=1, replica_groups=mesh['row'=4,'col'=8] {'col'}, dimensions={1} | all-to-all | bytes 65536 | tf_op jit(solution)/shard_map/all_to_all | solution.py:95
  113.8 4.7 %all-to-all-start.2 = ((f32[1,8,1,8,128,128]{5,4,3,2,0,1:T(8,128)}), f32[1,8,1,8,128,128]{5,4,3,2,0,1:T(8,128)}, u32[]{:S(2)}, u32[]{:S(2)}) async-start(f32[1,8,1,8,128,128]{5,4,3,2,0,1:T(8,128)} %bitcast.92), calls=%async_computation.2 | async-start | bytes 8388608 | tf_op jit(solution)/shard_map/all_to_all | solution.py:94
  118.6 15.7 %while.27 = (s32[]{:T(128)}, f32[8,1024,2]{1,2,0:T(2,128)S(1)}, s32[8,1024]{1,0:T(8,128)S(1)}, f32[8,1024,2]{1,2,0:T(2,128)S(1)}, s32[]{:T(128)}) while((s32[]{:T(128)}, f32[8,1024,2]{1,2,0:T(2,128)S(1)}, s32[8,1024]{1,0:T(8,128)S(1)}, f32[8,1024,2]{1,2,0:T(2,128)S(1)}, s32[]{:T(128)}) %tuple.59), condition=%wide.region_3.4_spmd.clone, body=%wide.region_2.3_spmd.clone.sunk | while | flops 26214400 | bytes 29761 | solution.py:65
  118.6 1.9 fusion.37
  120.6 1.9 fusion.37
  122.6 1.9 fusion.37
  124.5 1.9 fusion.37
  126.5 1.9 fusion.37
  128.4 1.9 fusion.37
  130.4 1.9 fusion.37
  132.4 1.9 fusion.37
  134.4 65.0 %all-reduce.2 = (f32[1024]{0:T(1024)S(1)}, f32[1024]{0:T(1024)S(1)}) all-reduce(f32[1024]{0:T(1024)S(1)} %bitcast.113, f32[1024]{0:T(1024)S(1)} %bitcast.112), channel_id=1, replica_groups=mesh['row'=4,'col'=8] {'row','col'}, use_global_device_ids=true, to_apply=%region_5.6 | all-reduce | flops 2048 | bytes 16384 | tf_op jit(solution)/shard_map/psum | solution.py:102
  199.3 0.6 maximum_divide_fusion
  200.0 4.7 %copy.64 = f32[1,1,8,8,128,128]{5,4,3,2,1,0:T(8,128)} copy(f32[1,1,8,8,128,128]{5,4,3,2,1,0:T(8,128)} %bitcast.9) | data formatting | bytes 8388608
  204.7 0.6 copy.65
  (51 shorter events, 0.8 us)
Async XLA Ops:
  0.6 44.7 %all-to-all-start.1 = ((s32[1,1,8,8,128]{4,3,1,0,2:T(8,128)}), s32[1,1,8,8,128]{4,3,1,0,2:T(8,128)S(1)}, u32[]{:S(2)}, u32[]{:S(2)}) async-start(s32[1,1,8,8,128]{4,3,1,0,2:T(8,128)} %bitcast.95), calls=%async_computation.1 | async-start | bytes 65536 | tf_op jit(solution)/shard_map/all_to_all | solution.py:79
  45.4 9.0 %all-to-all-start = ((s32[1,1,8,8,128]{4,3,1,0,2:T(8,128)}), s32[1,1,8,8,128]{4,3,1,0,2:T(8,128)S(1)}, u32[]{:S(2)}, u32[]{:S(2)}) async-start(s32[1,1,8,8,128]{4,3,1,0,2:T(8,128)} %bitcast.97), calls=%async_computation | async-start | bytes 65536 | tf_op jit(solution)/shard_map/all_to_all | solution.py:78
  98.5 8.1 %all-to-all-start.4 = ((f32[1,8,1,8,128]{4,3,2,0,1:T(8,128)}), f32[1,8,1,8,128]{4,3,2,0,1:T(8,128)S(1)}, u32[]{:S(2)}, u32[]{:S(2)}) async-start(f32[1,8,1,8,128]{4,3,2,0,1:T(8,128)} %bitcast.65), calls=%async_computation.4 | async-start | bytes 65536 | tf_op jit(solution)/shard_map/all_to_all | solution.py:96
  113.8 4.7 %copy-start = (s32[1,1,8,8,128]{4,3,2,1,0:T(8,128)S(1)}, s32[1,1,8,8,128]{4,3,2,1,0:T(8,128)}, u32[]{:S(2)}) copy-start(s32[1,1,8,8,128]{4,3,2,1,0:T(8,128)} %param.13) | copy-start | bytes 98308
  113.8 4.7 %copy-start.1 = (s32[1,1,8,8,128]{4,3,2,1,0:T(8,128)S(1)}, s32[1,1,8,8,128]{4,3,2,1,0:T(8,128)}, u32[]{:S(2)}) copy-start(s32[1,1,8,8,128]{4,3,2,1,0:T(8,128)} %param.12) | copy-start | bytes 98308
  113.8 86.2 %all-to-all-start.2 = ((f32[1,8,1,8,128,128]{5,4,3,2,0,1:T(8,128)}), f32[1,8,1,8,128,128]{5,4,3,2,0,1:T(8,128)}, u32[]{:S(2)}, u32[]{:S(2)}) async-start(f32[1,8,1,8,128,128]{5,4,3,2,0,1:T(8,128)} %bitcast.92), calls=%async_computation.2 | async-start | bytes 8388608 | tf_op jit(solution)/shard_map/all_to_all | solution.py:94
where the time goes:
time: 206 us; the launch traced here: 205 us
  blocking collectives  108 us (52%)
  matrix products  56.2 us (27%)
  starting transfers between devices  17.4 us (8%)
  local copies, waits for them, and re-layouts  9.87 us (5%)
  waiting for transfers between devices  9.58 us (5%)
  other arithmetic  2.17 us (1%)
    psum x1, blocking collectives, local(): lax.psum((local_sums[:, 0], local_sums[:, 1]), ('row', 'col'))  65 us
    dot_general x8, matrix products, tile_one_block(): jnp.dot(matched, flat_payload, precision=lax.Precision.HIGHEST, preferred...  23.5 us
    dot_general x8, matrix products, tile_one_block(): jnp.dot(matched, side_columns, precision=lax.Precision.HIGHEST, preferred...  17.1 us
    all_gather x1, blocking collectives, local(): lax.all_gather(build_payload, 'row', axis=1, tiled=True)  16.7 us
    dot_general x8, matrix products, partition_one_block(): jnp.dot(onehot, values_here, precision=lax.Precision.HIGHEST, preferred_e...  15.5 us
    unnamed x1, blocking collectives  11.9 us
    all_gather x1, blocking collectives, local(): lax.all_gather(build_keys, 'row', axis=1, tiled=True)  7.57 us
    unnamed x13, local copies, waits for them, and re-layouts  7.22 us
  transfers between devices with their start and end apart: 4, of which 2 were waited for; matrix products, arithmetic and copies ran while one was open for 9% of the time, Pallas kernels for 0%

commit v1 on v0

v1 whole, which is shorter than its diff:
```python
import functools

import jax
import jax.numpy as jnp
from jax import lax
from jax.experimental import pallas as pl
from jax.experimental.pallas import tpu as pltpu
from jax.sharding import PartitionSpec as P

PARTS_SIZE = 1024
KEY_RANGE = 64
LANES = 128
MESH = pl.DeviceIdType.MESH


def dot_nt(a, b):
    return lax.dot_general(a, b, (((1,), (1,)), ((), ())), preferred_element_type=jnp.float32)


def gather_kernel(
    rows, cols, local_tiles,
    bkey_ref, bpart_ref, pay_ref, pkey_ref, ppart_ref,
    tables_ref, smalls_ref, place_ref, rate_ref,
    own, hist1, hist2,
    small_send, small_recv, table_send, table_recv, pass_send, pass_recv,
    h1_send, h1_recv, h2_send, h2_recv, local_sem,
):
    r, c = lax.axis_index("row"), lax.axis_index("col")
    n = rows * cols
    chips = cols // 2
    me = r * cols + c
    partner = c + 1 - 2 * lax.rem(c, 2)
    parity = lax.rem(c, 2)

    def peer(k):
        pr = lax.rem(r + k // cols, rows)
        pc = lax.rem(c + lax.rem(k, cols), cols)
        return pr, pc

    barrier = pltpu.get_barrier_semaphore()

    @pl.loop(1, n)
    def _(k):
        pl.semaphore_signal(barrier, inc=1, device_id=peer(k), device_id_type=MESH)

    tile_rows = bkey_ref.shape[-1]
    depth = local_tiles * KEY_RANGE
    table = jnp.zeros((depth, pay_ref.shape[-1]), jnp.float32)
    small = jnp.zeros((8, depth), jnp.float32)
    sub = lax.broadcasted_iota(jnp.int32, (depth, tile_rows), 0)
    srow = lax.broadcasted_iota(jnp.int32, (8, tile_rows), 0)
    slane = lax.broadcasted_iota(jnp.int32, (8, tile_rows), 1)
    lane = lax.broadcasted_iota(jnp.int32, (8, depth), 1)
    orow = lax.broadcasted_iota(jnp.int32, (8, depth), 0)
    weights = jnp.where(srow == 0, 1, jnp.where(srow == 1, slane, 0)).astype(jnp.float32)
    part_lane = jnp.zeros((8, depth), jnp.int32)
    first_lane = jnp.zeros((8, depth), jnp.int32)
    for t in range(local_tiles):
        keys = bkey_ref[0, t : t + 1, :]
        hot = (sub - t * KEY_RANGE == keys) & (keys >= 0)
        hot = jnp.where(hot, 1.0, 0.0)
        table += jnp.dot(hot, pay_ref[0, t], precision=lax.Precision.HIGHEST, preferred_element_type=jnp.float32)
        small += dot_nt(weights, hot)
        mine = lane // KEY_RANGE == t
        part_lane = jnp.where(mine, bpart_ref[0, t], part_lane)
        first_lane = jnp.where(mine, (r * local_tiles + t) * tile_rows, first_lane)
    own[...] = table
    count = small[0:1, :]
    place = (small[1:2, :] + count * first_lane[0:1, :].astype(jnp.float32)) / float(rows * local_tiles * tile_rows)
    code = part_lane * KEY_RANGE + lax.rem(lane, KEY_RANGE)
    smalls_ref[me] = jnp.where(
        orow == 0, count, jnp.where(orow == 1, place, jnp.where(orow == 2, code.astype(jnp.float32), 0.0))
    )
    keep = pltpu.make_async_copy(own, tables_ref.at[me], local_sem)
    keep.start()

    pl.semaphore_wait(barrier, n - 1)

    def small_copy(k):
        return pltpu.make_async_remote_copy(
            src_ref=smalls_ref.at[me], dst_ref=smalls_ref.at[me], send_sem=small_send, recv_sem=small_recv,
            device_id=peer(k), device_id_type=MESH)

    @pl.loop(1, n)
    def _(k):
        small_copy(k).start()

    def chip_peer(k):
        return lax.rem(r + k // chips, rows), lax.rem(c + 2 * lax.rem(k, chips), cols)

    def chip_source(k):
        return lax.rem(r + rows - k // chips, rows), lax.rem(c + cols - 2 * lax.rem(k, chips), cols)

    def table_copy(k):
        return pltpu.make_async_remote_copy(
            src_ref=own, dst_ref=tables_ref.at[me], send_sem=table_send, recv_sem=table_recv.at[k],
            device_id=chip_peer(k), device_id_type=MESH)

    @pl.loop(1, rows * chips)
    def _(k):
        table_copy(k).start()

    def pass_copy(slot, src):
        return pltpu.make_async_remote_copy(
            src_ref=src, dst_ref=tables_ref.at[slot], send_sem=pass_send, recv_sem=pass_recv,
            device_id=(r, partner), device_id_type=MESH)

    pass_copy(me, own).start()

    smalls_rest = smalls_ref.at[pl.ds(0, n - 1)]
    pltpu.make_async_copy(smalls_rest, smalls_rest, small_recv).wait()
    probe_tiles = pkey_ref.shape[3]
    hi_iota = lax.broadcasted_iota(jnp.int32, (PARTS_SIZE // LANES, LANES), 0)
    lo_iota = lax.broadcasted_iota(jnp.int32, (LANES, LANES), 0)
    groups = PARTS_SIZE // LANES

    def owner_step(o, acc):
        keys = pkey_ref[0, 0, o]
        parts = ppart_ref[0, 0, o]
        live = keys >= 0
        code = (parts * KEY_RANGE + keys).astype(jnp.float32)
        counts = jnp.zeros(keys.shape, jnp.float32)
        places = jnp.zeros(keys.shape, jnp.float32)
        for sr in range(rows):
            block = smalls_ref[sr * cols + o]
            tabs = [jnp.broadcast_to(block[j : j + 1, :], (probe_tiles, depth)) for j in range(3)]
            for t in range(local_tiles):
                index = jnp.where(live, keys, 0) + t * KEY_RANGE
                got = [jnp.take_along_axis(tab, index, axis=1) for tab in tabs]
                hit = live & (got[2] == code)
                counts += jnp.where(hit, got[0], 0.0)
                places += jnp.where(hit, got[1], 0.0)
        place_ref[o] = places
        big = jnp.floor(counts * (1.0 / 256.0))
        rest = counts - 256.0 * big
        alive = jnp.where(live, 1.0, 0.0)
        hi = parts // LANES
        lo = lax.rem(parts, LANES)
        for q in range(probe_tiles):
            hot_hi = hi_iota == hi[q : q + 1, :]
            lhs = jnp.concatenate(
                [jnp.where(hot_hi, v[q : q + 1, :], 0.0) for v in (rest, big, alive)]
                + [jnp.zeros((groups, LANES), jnp.float32)], axis=0)
            rhs = jnp.where(lo_iota == lo[q : q + 1, :], 1.0, 0.0)
            acc += dot_nt(lhs.astype(jnp.bfloat16), rhs.astype(jnp.bfloat16))
        return acc

    acc = lax.fori_loop(0, cols, owner_step, jnp.zeros((4 * groups, LANES), jnp.float32))
    hist1[c, 0:groups, :] = acc[0:groups] + 256.0 * acc[groups : 2 * groups]
    hist1[c, groups : 2 * groups, :] = acc[2 * groups : 3 * groups]

    def h1_copy(k):
        return pltpu.make_async_remote_copy(
            src_ref=hist1.at[c], dst_ref=hist1.at[c], send_sem=h1_send, recv_sem=h1_recv,
            device_id=(r, lax.rem(c + k, cols)), device_id_type=MESH)

    @pl.loop(1, cols)
    def _(k):
        h1_copy(k).start()

    @pl.loop(1, rows * chips)
    def _(k):
        sr, sc = chip_source(k)
        slot = sr * cols + sc
        pltpu.make_async_copy(tables_ref.at[slot], tables_ref.at[slot], table_recv.at[k]).wait()
        pass_copy(slot, tables_ref.at[slot]).start()

    hist1_rest = hist1.at[pl.ds(0, cols - 1)]
    pltpu.make_async_copy(hist1_rest, hist1_rest, h1_recv).wait()
    hist2[r] = functools.reduce(lambda a, b: a + b, [hist1[j] for j in range(cols)])

    @pl.loop(1, rows)
    def _(k):
        pltpu.make_async_remote_copy(
            src_ref=hist2.at[r], dst_ref=hist2.at[r], send_sem=h2_send, recv_sem=h2_recv,
            device_id=(lax.rem(r + k, rows), c), device_id_type=MESH).start()

    hist2_rest = hist2.at[pl.ds(0, rows - 1)]
    pltpu.make_async_copy(hist2_rest, hist2_rest, h2_recv).wait()
    total = functools.reduce(lambda a, b: a + b, [hist2[j] for j in range(rows)])
    rate_ref[...] = total[0:groups] / jnp.maximum(total[groups : 2 * groups], 1.0)

    keep.wait()
    pltpu.make_async_copy(smalls_rest, smalls_rest, small_send).wait()
    pltpu.make_async_copy(hist1_rest, hist1_rest, h1_send).wait()
    pltpu.make_async_copy(hist2_rest, hist2_rest, h2_send).wait()
    others = tables_ref.at[pl.ds(0, rows * chips - 1)]
    pltpu.make_async_copy(others, others, table_send).wait()
    passed = tables_ref.at[pl.ds(0, rows * chips)]
    pltpu.make_async_copy(passed, passed, pass_send).wait()
    pltpu.make_async_copy(passed, passed, pass_recv).wait()


def join_kernel(tables_ref, smalls_ref, pkey_ref, ppart_ref, place_ref, rate_ref, joined_ref, place_out, rate_out):
    rows, _, depth, width = tables_ref.shape
    probe_tiles, tile_rows = pkey_ref.shape[3], pkey_ref.shape[4]
    table = tables_ref[...].reshape(rows * depth, width)
    high = table.astype(jnp.bfloat16)
    low = (table - high.astype(jnp.float32)).astype(jnp.bfloat16)
    both = jnp.concatenate([high, low], axis=1)
    keys = pkey_ref[0, 0, 0]
    code = jnp.where(keys >= 0, ppart_ref[0, 0, 0] * KEY_RANGE + keys, -1).astype(jnp.float32)
    code = code.T
    for q in range(probe_tiles):
        wide = jnp.broadcast_to(code[:, q : q + 1], (tile_rows, depth))
        hot = jnp.concatenate(
            [jnp.where(wide == smalls_ref[s, 0, 2:3, :], 1.0, 0.0).astype(jnp.bfloat16) for s in range(rows)], axis=1)
        out = jnp.dot(hot, both, preferred_element_type=jnp.float32)
        joined_ref[0, 0, 0, q] = out[:, :width] + out[:, width:]
    place_out[...] = place_ref[...].reshape(place_out.shape)
    rate_out[...] = rate_ref[...]


def local(build_key, build_part, build_payload, probe_key, probe_part):
    rows, cols = lax.axis_size("row"), lax.axis_size("col")
    n = rows * cols
    local_tiles = build_key.shape[1]
    width = build_payload.shape[-1]
    owners, probe_tiles, tile_rows = probe_key.shape[2:]
    depth = local_tiles * KEY_RANGE
    groups = PARTS_SIZE // LANES
    vmem = pl.BlockSpec(memory_space=pltpu.VMEM)
    dma = pltpu.SemaphoreType.DMA
    f32 = jnp.float32
    tables, smalls, places, rate = pl.pallas_call(
        functools.partial(gather_kernel, rows, cols, local_tiles),
        out_shape=(
            jax.ShapeDtypeStruct((n, depth, width), f32),
            jax.ShapeDtypeStruct((n, 8, depth), f32),
            jax.ShapeDtypeStruct((owners, probe_tiles, tile_rows), f32),
            jax.ShapeDtypeStruct((groups, LANES), f32),
        ),
        in_specs=[vmem, pl.BlockSpec(memory_space=pltpu.SMEM), vmem, vmem, vmem],
        out_specs=(vmem, vmem, vmem, vmem),
        scratch_shapes=[
            pltpu.VMEM((depth, width), f32),
            pltpu.VMEM((cols, 2 * groups, LANES), f32),
            pltpu.VMEM((rows, 2 * groups, LANES), f32),
            dma, dma, dma, dma((rows * (cols // 2),)), dma, dma,
            dma, dma, dma, dma, dma,
        ],
        compiler_params=pltpu.CompilerParams(
            collective_id=0, has_side_effects=True, vmem_limit_bytes=40 * 1024 * 1024
        ),
    )(build_key, build_part, build_payload, probe_key, probe_part)
    tables = tables.reshape(rows, cols, depth, width)
    smalls = smalls.reshape(rows, cols, 8, depth)
    joined, placed, rate = pl.pallas_call(
        join_kernel,
        grid=(owners,),
        out_shape=(
            jax.ShapeDtypeStruct((1, 1, owners, probe_tiles, tile_rows, width), f32),
            jax.ShapeDtypeStruct((1, 1, owners, probe_tiles, tile_rows), f32),
            jax.ShapeDtypeStruct((groups, LANES), f32),
        ),
        in_specs=[
            pl.BlockSpec((rows, 1, depth, width), lambda i: (0, i, 0, 0)),
            pl.BlockSpec((rows, 1, 8, depth), lambda i: (0, i, 0, 0)),
            pl.BlockSpec((1, 1, 1, probe_tiles, tile_rows), lambda i: (0, 0, i, 0, 0)),
            pl.BlockSpec((1, 1, 1, probe_tiles, tile_rows), lambda i: (0, 0, i, 0, 0)),
            pl.BlockSpec((1, probe_tiles, tile_rows), lambda i: (i, 0, 0)),
            pl.BlockSpec((groups, LANES), lambda i: (0, 0)),
        ],
        out_specs=(
            pl.BlockSpec((1, 1, 1, probe_tiles, tile_rows, width), lambda i: (0, 0, i, 0, 0, 0)),
            pl.BlockSpec((1, 1, 1, probe_tiles, tile_rows), lambda i: (0, 0, i, 0, 0)),
            pl.BlockSpec((groups, LANES), lambda i: (0, 0)),
        ),
    )(tables, smalls, probe_key, probe_part, places, rate)
    return joined, placed, rate.reshape(PARTS_SIZE)


def solution(mesh):
    return jax.shard_map(
        local,
        mesh=mesh,
        in_specs=(
            P("col", "row", None),
            P("col", "row"),
            P("col", "row", None, None),
            P("row", "col", None, None, None),
            P("row", "col", None, None, None),
        ),
        out_specs=(P("row", "col", None, None, None, None), P("row", "col", None, None, None), P()),
        check_vma=False,
    )
```

time: 206 us -> 55.6 us (0.27)
  blocking collectives: 108 us -> 0 us
  matrix products: 56.2 us -> 0 us
  Pallas kernels: 0 us -> 47.6 us
  starting transfers between devices: 17.4 us -> 0 us
  waiting for transfers between devices: 9.58 us -> 0 us
  local copies, waits for them, and re-layouts: 9.87 us -> 6.92 us
  other arithmetic: 2.17 us -> 0 us
    psum x1 -> x0, blocking collectives: 65 us -> none  [local(): lax.psum((local_sums[:, 0], local_sums[:, 1]), ('row', 'col'))]
    dot_general x24 -> x0, matrix products: 56.2 us -> none  [the longest x8 23.5 us: tile_one_block(): jnp.dot(matched, flat_payload, precision=lax.Precision.HIGHEST, preferred...]
    pallas_call x0 -> x2, Pallas kernels: none -> 47.6 us  [the longest x1 39.3 us: local(): pl.pallas_call(functools.partial(gather_kernel, rows, cols, local_tiles),...]
    all_gather x2 -> x0, blocking collectives: 24.3 us -> none  [the longest x1 16.7 us: local(): lax.all_gather(build_payload, 'row', axis=1, tiled=True)]
    all_to_all x4 -> x0, starting transfers between devices: 17.4 us -> none  [the longest x1 5.21 us: local(): lax.all_to_all(probe_part, 'col', split_axis=2, concat_axis=1, tiled=True)]
    unnamed x1 -> x0, blocking collectives: 11.9 us -> none
    all_to_all x4 -> x0, waiting for transfers between devices: 9.58 us -> none  [the longest x1 4.82 us: local(): lax.all_to_all(probe_key, 'col', split_axis=2, concat_axis=1, tiled=True)]
    all_to_all x1 -> x0, blocking collectives: 7.2 us -> none  [local(): lax.all_to_all(places, 'col', split_axis=1, concat_axis=2, tiled=True)]
  transfers between devices with their start and end apart: 4 -> 0, of which waited for: 2 -> 0; matrix products, arithmetic and copies ran while one was open for 9% -> 0% of each run, Pallas kernels for 0% -> 0%
where the time goes in v1:
time: 55.6 us; the launch traced here: 55.2 us
  Pallas kernels  47.6 us (86%)
  local copies, waits for them, and re-layouts  6.92 us (12%)
  between operations  0.66 us (1%)
    pallas_call x1, Pallas kernels, local(): pl.pallas_call(functools.partial(gather_kernel, rows, cols, local_tiles),...  39.3 us
    pallas_call x1, Pallas kernels, local(): pl.pallas_call(join_kernel, grid=(owners,), out_shape=(jax.ShapeDtypeStru...  8.23 us
    unnamed x18, local copies, waits for them, and re-layouts  6.92 us

profile of v1, /device:TPU:0, one launch (start us, length us, event | category | flops | bytes accessed | tf_op | source)
XLA Modules:
  0.0 55.2 jit_solution(17968437144575588940)
XLA Ops:
  0.6 0.0 copy-start.1
  0.6 0.7 %copy-done.1 = s32[1,1,8,8,128]{4,3,2,1,0:T(8,128)S(1)} copy-done((s32[1,1,8,8,128]{4,3,2,1,0:T(8,128)S(1)}, s32[1,1,8,8,128]{4,3,2,1,0:T(8,128)}, u32[]{:S(2)}) %copy-start.1) | copy-done | bytes 32792
  1.4 0.0 copy-start.2
  1.4 0.8 %copy-done.2 = s32[1,1,8,8,128]{4,3,2,1,0:T(8,128)S(1)} copy-done((s32[1,1,8,8,128]{4,3,2,1,0:T(8,128)S(1)}, s32[1,1,8,8,128]{4,3,2,1,0:T(8,128)}, u32[]{:S(2)}) %copy-start.2) | copy-done | bytes 32792
  2.1 0.0 copy-start.4
  2.2 0.9 %copy-done.4 = f32[1,2,128,128]{3,2,1,0:T(8,128)S(1)} copy-done((f32[1,2,128,128]{3,2,1,0:T(8,128)S(1)}, f32[1,2,128,128]{3,2,1,0:T(8,128)}, u32[]{:S(2)}) %copy-start.4) | copy-done | bytes 131096
  3.1 0.0 copy-start.7
  3.1 0.7 %copy-done.7 = s32[1,2,128]{2,1,0:T(2,128)S(1)} copy-done((s32[1,2,128]{2,1,0:T(2,128)S(1)}, s32[1,2,128]{2,1,0:T(2,128)}, u32[]{:S(2)}) %copy-start.7) | copy-done | bytes 1048
  3.7 0.0 copy-start.8
  3.7 0.7 %copy-done.8 = s32[1,2]{1,0:T(1,128)S(1)} copy-done((s32[1,2]{1,0:T(1,128)S(1)}, s32[1,2]{1,0:T(1,128)}, u32[]{:S(2)}) %copy-start.8) | copy-done | bytes 32
  4.4 39.3 %shard_map.76 = (f32[32,128,128]{2,1,0:T(8,128)S(1)}, f32[32,8,128]{2,1,0:T(8,128)S(1)}, f32[8,8,128]{2,1,0:T(8,128)S(1)}, f32[8,128]{1,0:T(8,128)S(1)}) custom-call(s32[1,2,128]{2,1,0:T(2,128)S(1)} %copy-done.7, s32[1,2]{1,0:T(1,128)S(1)} %copy-done.8, f32[1,2,128,128]{3,2,1,0:T(8,128)S(1)} %copy-done.4, s32[1,1,8,8,128]{4,3,2,1,0:T(8,128)S(1)} %copy-done.1, ...), custom_call_target="tpu_custom_call" | custom-call | tf_op jit(solution)/shard_map/pallas_call | solution.py:225
  43.7 0.0 copy-start
  43.8 1.3 %copy-done = f32[32,128,128]{2,1,0:T(8,128)} copy-done((f32[32,128,128]{2,1,0:T(8,128)}, f32[32,128,128]{2,1,0:T(8,128)S(1)}, u32[]{:S(2)}) %copy-start) | copy-done | bytes 2097176
  45.1 0.0 copy-start.3
  45.1 0.6 %copy-done.3 = f32[32,8,128]{2,1,0:T(8,128)} copy-done((f32[32,8,128]{2,1,0:T(8,128)}, f32[32,8,128]{2,1,0:T(8,128)S(1)}, u32[]{:S(2)}) %copy-start.3) | copy-done | bytes 131096
  45.7 0.0 copy-start.5
  45.7 0.6 %copy-done.5 = f32[8,8,128]{2,1,0:T(8,128)} copy-done((f32[8,8,128]{2,1,0:T(8,128)}, f32[8,8,128]{2,1,0:T(8,128)S(1)}, u32[]{:S(2)}) %copy-start.5) | copy-done | bytes 32792
  46.3 0.0 copy-start.6
  46.3 0.6 %copy-done.6 = f32[8,128]{1,0:T(8,128)} copy-done((f32[8,128]{1,0:T(8,128)}, f32[8,128]{1,0:T(8,128)S(1)}, u32[]{:S(2)}) %copy-start.6) | copy-done | bytes 4120
  46.9 8.2 %shard_map.77 = (f32[1,1,8,8,128,128]{5,4,3,2,1,0:T(8,128)}, f32[1,1,8,8,128]{4,3,2,1,0:T(8,128)}, f32[8,128]{1,0:T(8,128)}) custom-call(f32[4,8,128,128]{3,2,1,0:T(8,128)} %bitcast.3, f32[4,8,8,128]{3,2,1,0:T(8,128)} %bitcast.4, s32[1,1,8,8,128]{4,3,2,1,0:T(8,128)} %pkey_ref.3, s32[1,1,8,8,128]{4,3,2,1,0:T(8,128)} %ppart_ref.3, f32[8,8,128]{2,1,0:T(8,128)} %copy-done.5, ...), custom_call_target="tpu_custom_call" | custom-call | tf_op jit(solution)/shard_map/pallas_call | solution.py:248
Async XLA Ops:
  0.6 0.8 %copy-start.1 = (s32[1,1,8,8,128]{4,3,2,1,0:T(8,128)S(1)}, s32[1,1,8,8,128]{4,3,2,1,0:T(8,128)}, u32[]{:S(2)}) copy-start(s32[1,1,8,8,128]{4,3,2,1,0:T(8,128)} %pkey_ref.3) | copy-start | bytes 98308
  1.4 0.8 %copy-start.2 = (s32[1,1,8,8,128]{4,3,2,1,0:T(8,128)S(1)}, s32[1,1,8,8,128]{4,3,2,1,0:T(8,128)}, u32[]{:S(2)}) copy-start(s32[1,1,8,8,128]{4,3,2,1,0:T(8,128)} %ppart_ref.3) | copy-start | bytes 98308
  2.1 0.9 %copy-start.4 = (f32[1,2,128,128]{3,2,1,0:T(8,128)S(1)}, f32[1,2,128,128]{3,2,1,0:T(8,128)}, u32[]{:S(2)}) copy-start(f32[1,2,128,128]{3,2,1,0:T(8,128)} %pay_ref.1) | copy-start | bytes 393220
  3.1 0.7 %copy-start.7 = (s32[1,2,128]{2,1,0:T(2,128)S(1)}, s32[1,2,128]{2,1,0:T(2,128)}, u32[]{:S(2)}) copy-start(s32[1,2,128]{2,1,0:T(2,128)} %bkey_ref.1) | copy-start | bytes 3076
  3.7 0.7 %copy-start.8 = (s32[1,2]{1,0:T(1,128)S(1)}, s32[1,2]{1,0:T(1,128)}, u32[]{:S(2)}) copy-start(s32[1,2]{1,0:T(1,128)} %bpart_ref.1) | copy-start | bytes 28
  43.7 1.3 %copy-start = (f32[32,128,128]{2,1,0:T(8,128)}, f32[32,128,128]{2,1,0:T(8,128)S(1)}, u32[]{:S(2)}) copy-start(f32[32,128,128]{2,1,0:T(8,128)S(1)} %get-tuple-element.10) | copy-start | bytes 6291460
  45.1 0.7 %copy-start.3 = (f32[32,8,128]{2,1,0:T(8,128)}, f32[32,8,128]{2,1,0:T(8,128)S(1)}, u32[]{:S(2)}) copy-start(f32[32,8,128]{2,1,0:T(8,128)S(1)} %get-tuple-element.11) | copy-start | bytes 393220
  45.7 0.6 %copy-start.5 = (f32[8,8,128]{2,1,0:T(8,128)}, f32[8,8,128]{2,1,0:T(8,128)S(1)}, u32[]{:S(2)}) copy-start(f32[8,8,128]{2,1,0:T(8,128)S(1)} %get-tuple-element.12.place_ref) | copy-start | bytes 98308
  46.3 0.6 %copy-start.6 = (f32[8,128]{1,0:T(8,128)}, f32[8,128]{1,0:T(8,128)S(1)}, u32[]{:S(2)}) copy-start(f32[8,128]{1,0:T(8,128)S(1)} %get-tuple-element.13.rate_ref) | copy-start | bytes 12292

commit v2 on v1

--- a/solution.py
+++ b/solution.py
@@ -19,9 +19,10 @@
 
 def gather_kernel(
     rows, cols, local_tiles,
+    bkey_hbm, bpart_hbm, pay_hbm, pkey_hbm, ppart_hbm,
+    tables_ref, smalls_ref, place_ref, rate_ref,
     bkey_ref, bpart_ref, pay_ref, pkey_ref, ppart_ref,
-    tables_ref, smalls_ref, place_ref, rate_ref,
-    own, hist1, hist2,
+    own, hist1, hist2, in_sem,
     small_send, small_recv, table_send, table_recv, pass_send, pass_recv,
     h1_send, h1_recv, h2_send, h2_recv, local_sem,
 ):
@@ -37,12 +38,20 @@
         pc = lax.rem(c + lax.rem(k, cols), cols)
         return pr, pc
 
+    pairs = (
+        (bkey_hbm, bkey_ref), (bpart_hbm, bpart_ref), (pay_hbm, pay_ref), (pkey_hbm, pkey_ref), (ppart_hbm, ppart_ref)
+    )
+    loads = [pltpu.make_async_copy(src, dst, in_sem.at[i]) for i, (src, dst) in enumerate(pairs)]
+    for load in loads:
+        load.start()
     barrier = pltpu.get_barrier_semaphore()
 
     @pl.loop(1, n)
     def _(k):
         pl.semaphore_signal(barrier, inc=1, device_id=peer(k), device_id_type=MESH)
 
+    for load in loads[:3]:
+        load.wait()
     tile_rows = bkey_ref.shape[-1]
     depth = local_tiles * KEY_RANGE
     table = jnp.zeros((depth, pay_ref.shape[-1]), jnp.float32)
@@ -107,6 +116,8 @@
 
     pass_copy(me, own).start()
 
+    for load in loads[3:]:
+        load.wait()
     smalls_rest = smalls_ref.at[pl.ds(0, n - 1)]
     pltpu.make_async_copy(smalls_rest, smalls_rest, small_recv).wait()
     probe_tiles = pkey_ref.shape[3]
@@ -136,14 +147,14 @@
         alive = jnp.where(live, 1.0, 0.0)
         hi = parts // LANES
         lo = lax.rem(parts, LANES)
+        lhs, rhs = [], []
         for q in range(probe_tiles):
             hot_hi = hi_iota == hi[q : q + 1, :]
-            lhs = jnp.concatenate(
+            lhs.append(jnp.concatenate(
                 [jnp.where(hot_hi, v[q : q + 1, :], 0.0) for v in (rest, big, alive)]
-                + [jnp.zeros((groups, LANES), jnp.float32)], axis=0)
-            rhs = jnp.where(lo_iota == lo[q : q + 1, :], 1.0, 0.0)
-            acc += dot_nt(lhs.astype(jnp.bfloat16), rhs.astype(jnp.bfloat16))
-        return acc
+                + [jnp.zeros((groups, LANES), jnp.float32)], axis=0).astype(jnp.bfloat16))
+            rhs.append(jnp.where(lo_iota == lo[q : q + 1, :], 1.0, 0.0).astype(jnp.bfloat16))
+        return acc + dot_nt(jnp.concatenate(lhs, axis=1), jnp.concatenate(rhs, axis=1))
 
     acc = lax.fori_loop(0, cols, owner_step, jnp.zeros((4 * groups, LANES), jnp.float32))
     hist1[c, 0:groups, :] = acc[0:groups] + 256.0 * acc[groups : 2 * groups]
@@ -192,22 +203,25 @@
 
 
 def join_kernel(tables_ref, smalls_ref, pkey_ref, ppart_ref, place_ref, rate_ref, joined_ref, place_out, rate_out):
+    owner = pl.program_id(0)
     rows, _, depth, width = tables_ref.shape
     probe_tiles, tile_rows = pkey_ref.shape[3], pkey_ref.shape[4]
-    table = tables_ref[...].reshape(rows * depth, width)
+    table = tables_ref[:, owner].reshape(rows * depth, width)
     high = table.astype(jnp.bfloat16)
     low = (table - high.astype(jnp.float32)).astype(jnp.bfloat16)
     both = jnp.concatenate([high, low], axis=1)
     keys = pkey_ref[0, 0, 0]
     code = jnp.where(keys >= 0, ppart_ref[0, 0, 0] * KEY_RANGE + keys, -1).astype(jnp.float32)
     code = code.T
+    wanted = [smalls_ref[s, owner, 2:3, :] for s in range(rows)]
+    hot = []
     for q in range(probe_tiles):
         wide = jnp.broadcast_to(code[:, q : q + 1], (tile_rows, depth))
-        hot = jnp.concatenate(
-            [jnp.where(wide == smalls_ref[s, 0, 2:3, :], 1.0, 0.0).astype(jnp.bfloat16) for s in range(rows)], axis=1)
-        out = jnp.dot(hot, both, preferred_element_type=jnp.float32)
-        joined_ref[0, 0, 0, q] = out[:, :width] + out[:, width:]
-    place_out[...] = place_ref[...].reshape(place_out.shape)
+        hot.append(jnp.concatenate(
+            [jnp.where(wide == want, 1.0, 0.0).astype(jnp.bfloat16) for want in wanted], axis=1))
+    out = jnp.dot(jnp.concatenate(hot, axis=0), both, preferred_element_type=jnp.float32)
+    joined_ref[0, 0, 0] = (out[:, :width] + out[:, width:]).reshape(probe_tiles, tile_rows, width)
+    place_out[...] = place_ref[owner].reshape(place_out.shape)
     rate_out[...] = rate_ref[...]
 
 
@@ -230,12 +244,18 @@
             jax.ShapeDtypeStruct((owners, probe_tiles, tile_rows), f32),
             jax.ShapeDtypeStruct((groups, LANES), f32),
         ),
-        in_specs=[vmem, pl.BlockSpec(memory_space=pltpu.SMEM), vmem, vmem, vmem],
+        in_specs=[pl.BlockSpec(memory_space=pltpu.HBM)] * 5,
         out_specs=(vmem, vmem, vmem, vmem),
         scratch_shapes=[
+            pltpu.VMEM(build_key.shape, build_key.dtype),
+            pltpu.SMEM(build_part.shape, build_part.dtype),
+            pltpu.VMEM(build_payload.shape, f32),
+            pltpu.VMEM(probe_key.shape, probe_key.dtype),
+            pltpu.VMEM(probe_part.shape, probe_part.dtype),
             pltpu.VMEM((depth, width), f32),
             pltpu.VMEM((cols, 2 * groups, LANES), f32),
             pltpu.VMEM((rows, 2 * groups, LANES), f32),
+            dma((5,)),
             dma, dma, dma, dma((rows * (cols // 2),)), dma, dma,
             dma, dma, dma, dma, dma,
         ],
@@ -254,18 +274,19 @@
             jax.ShapeDtypeStruct((groups, LANES), f32),
         ),
         in_specs=[
-            pl.BlockSpec((rows, 1, depth, width), lambda i: (0, i, 0, 0)),
-            pl.BlockSpec((rows, 1, 8, depth), lambda i: (0, i, 0, 0)),
+            vmem,
+            vmem,
             pl.BlockSpec((1, 1, 1, probe_tiles, tile_rows), lambda i: (0, 0, i, 0, 0)),
             pl.BlockSpec((1, 1, 1, probe_tiles, tile_rows), lambda i: (0, 0, i, 0, 0)),
-            pl.BlockSpec((1, probe_tiles, tile_rows), lambda i: (i, 0, 0)),
-            pl.BlockSpec((groups, LANES), lambda i: (0, 0)),
+            vmem,
+            vmem,
         ],
         out_specs=(
             pl.BlockSpec((1, 1, 1, probe_tiles, tile_rows, width), lambda i: (0, 0, i, 0, 0, 0)),
             pl.BlockSpec((1, 1, 1, probe_tiles, tile_rows), lambda i: (0, 0, i, 0, 0)),
             pl.BlockSpec((groups, LANES), lambda i: (0, 0)),
         ),
+        compiler_params=pltpu.CompilerParams(vmem_limit_bytes=24 * 1024 * 1024),
     )(tables, smalls, probe_key, probe_part, places, rate)
     return joined, placed, rate.reshape(PARTS_SIZE)
 

time: 55.6 us -> 49.9 us (0.90)
  local copies, waits for them, and re-layouts: 6.92 us -> 3.75 us
  Pallas kernels: 47.6 us -> 45.2 us
    unnamed x18 -> x10, local copies, waits for them, and re-layouts: 6.92 us -> 3.75 us
    pallas_call x1, Pallas kernels: 8.23 us -> 6.12 us  [local(): pl.pallas_call(join_kernel, grid=(owners,), out_shape=(jax.ShapeDtypeStru...]
where the time goes in v2:
time: 49.9 us; the launch traced here: 49.6 us
  Pallas kernels  45.2 us (91%)
  local copies, waits for them, and re-layouts  3.75 us (8%)
  between operations  0.65 us (1%)
    pallas_call x1, Pallas kernels, local(): pl.pallas_call(functools.partial(gather_kernel, rows, cols, local_tiles),...  39.1 us
    pallas_call x1, Pallas kernels, local(): pl.pallas_call(join_kernel, grid=(owners,), out_shape=(jax.ShapeDtypeStru...  6.12 us
    unnamed x10, local copies, waits for them, and re-layouts  3.75 us

profile of v2, /device:TPU:0, one launch (start us, length us, event | category | flops | bytes accessed | tf_op | source)
XLA Modules:
  0.0 49.6 jit_solution(3216409863884897559)
XLA Ops:
  0.6 0.0 copy-start
  0.6 0.7 %copy-done = s32[1,1,8,8,128]{4,3,2,1,0:T(8,128)S(1)} copy-done((s32[1,1,8,8,128]{4,3,2,1,0:T(8,128)S(1)}, s32[1,1,8,8,128]{4,3,2,1,0:T(8,128)}, u32[]{:S(2)}) %copy-start) | copy-done | bytes 32792
  1.4 0.0 copy-start.1
  1.4 0.8 %copy-done.1 = s32[1,1,8,8,128]{4,3,2,1,0:T(8,128)S(1)} copy-done((s32[1,1,8,8,128]{4,3,2,1,0:T(8,128)S(1)}, s32[1,1,8,8,128]{4,3,2,1,0:T(8,128)}, u32[]{:S(2)}) %copy-start.1) | copy-done | bytes 32792
  2.1 0.0 copy-start.2
  2.2 0.9 %copy-done.2 = f32[1,2,128,128]{3,2,1,0:T(8,128)S(1)} copy-done((f32[1,2,128,128]{3,2,1,0:T(8,128)S(1)}, f32[1,2,128,128]{3,2,1,0:T(8,128)}, u32[]{:S(2)}) %copy-start.2) | copy-done | bytes 131096
  3.1 0.0 copy-start.3
  3.1 0.7 %copy-done.3 = s32[1,2,128]{2,1,0:T(2,128)S(1)} copy-done((s32[1,2,128]{2,1,0:T(2,128)S(1)}, s32[1,2,128]{2,1,0:T(2,128)}, u32[]{:S(2)}) %copy-start.3) | copy-done | bytes 1048
  3.7 0.0 copy-start.4
  3.7 0.7 %copy-done.4 = s32[1,2]{1,0:T(1,128)S(1)} copy-done((s32[1,2]{1,0:T(1,128)S(1)}, s32[1,2]{1,0:T(1,128)}, u32[]{:S(2)}) %copy-start.4) | copy-done | bytes 32
  4.4 39.1 %shard_map.76 = (f32[32,128,128]{2,1,0:T(8,128)S(1)}, f32[32,8,128]{2,1,0:T(8,128)S(1)}, f32[8,8,128]{2,1,0:T(8,128)S(1)}, f32[8,128]{1,0:T(8,128)S(1)}) custom-call(s32[1,2,128]{2,1,0:T(2,128)S(1)} %copy-done.3, s32[1,2]{1,0:T(1,128)S(1)} %copy-done.4, f32[1,2,128,128]{3,2,1,0:T(8,128)S(1)} %copy-done.2, s32[1,1,8,8,128]{4,3,2,1,0:T(8,128)S(1)} %copy-done, ...), custom_call_target="tpu_custom_call" | custom-call | tf_op jit(solution)/shard_map/pallas_call | solution.py:239
  43.5 6.1 %shard_map.77 = (f32[1,1,8,8,128,128]{5,4,3,2,1,0:T(8,128)}, f32[1,1,8,8,128]{4,3,2,1,0:T(8,128)}, f32[8,128]{1,0:T(8,128)}) custom-call(f32[4,8,128,128]{3,2,1,0:T(8,128)S(1)} %bitcast.3, f32[4,8,8,128]{3,2,1,0:T(8,128)S(1)} %bitcast.4, s32[1,1,8,8,128]{4,3,2,1,0:T(8,128)S(1)} %copy-done, s32[1,1,8,8,128]{4,3,2,1,0:T(8,128)S(1)} %copy-done.1, ...), custom_call_target="tpu_custom_call" | custom-call | tf_op jit(solution)/shard_map/pallas_call | solution.py:268
Async XLA Ops:
  0.6 0.8 %copy-start = (s32[1,1,8,8,128]{4,3,2,1,0:T(8,128)S(1)}, s32[1,1,8,8,128]{4,3,2,1,0:T(8,128)}, u32[]{:S(2)}) copy-start(s32[1,1,8,8,128]{4,3,2,1,0:T(8,128)} %pkey_ref.1) | copy-start | bytes 98308
  1.4 0.8 %copy-start.1 = (s32[1,1,8,8,128]{4,3,2,1,0:T(8,128)S(1)}, s32[1,1,8,8,128]{4,3,2,1,0:T(8,128)}, u32[]{:S(2)}) copy-start(s32[1,1,8,8,128]{4,3,2,1,0:T(8,128)} %ppart_ref.1) | copy-start | bytes 98308
  2.1 0.9 %copy-start.2 = (f32[1,2,128,128]{3,2,1,0:T(8,128)S(1)}, f32[1,2,128,128]{3,2,1,0:T(8,128)}, u32[]{:S(2)}) copy-start(f32[1,2,128,128]{3,2,1,0:T(8,128)} %pay_hbm.1) | copy-start | bytes 393220
  3.1 0.7 %copy-start.3 = (s32[1,2,128]{2,1,0:T(2,128)S(1)}, s32[1,2,128]{2,1,0:T(2,128)}, u32[]{:S(2)}) copy-start(s32[1,2,128]{2,1,0:T(2,128)} %bkey_hbm.1) | copy-start | bytes 3076
  3.7 0.7 %copy-start.4 = (s32[1,2]{1,0:T(1,128)S(1)}, s32[1,2]{1,0:T(1,128)}, u32[]{:S(2)}) copy-start(s32[1,2]{1,0:T(1,128)} %bpart_hbm.1) | copy-start | bytes 28

commit v3 on v2

--- a/solution.py
+++ b/solution.py
@@ -100,14 +100,18 @@
     def chip_source(k):
         return lax.rem(r + rows - k // chips, rows), lax.rem(c + cols - 2 * lax.rem(k, chips), cols)
 
-    def table_copy(k):
+    def table_copy(k, src, slot, target):
         return pltpu.make_async_remote_copy(
-            src_ref=own, dst_ref=tables_ref.at[me], send_sem=table_send, recv_sem=table_recv.at[k],
-            device_id=chip_peer(k), device_id_type=MESH)
-
-    @pl.loop(1, rows * chips)
-    def _(k):
-        table_copy(k).start()
+            src_ref=src, dst_ref=tables_ref.at[slot], send_sem=table_send, recv_sem=table_recv.at[k],
+            device_id=target, device_id_type=MESH)
+
+    @pl.loop(1, rows)
+    def _(i):
+        table_copy(i * chips, own, me, chip_peer(i * chips)).start()
+
+    @pl.loop(1, chips)
+    def _(j):
+        table_copy(j, own, me, chip_peer(j)).start()
 
     def pass_copy(slot, src):
         return pltpu.make_async_remote_copy(
@@ -120,6 +124,19 @@
         load.wait()
     smalls_rest = smalls_ref.at[pl.ds(0, n - 1)]
     pltpu.make_async_copy(smalls_rest, smalls_rest, small_recv).wait()
+
+    @pl.loop(1, rows)
+    def _(i):
+        sr, sc = chip_source(i * chips)
+        slot = sr * cols + sc
+        pltpu.make_async_copy(tables_ref.at[slot], tables_ref.at[slot], table_recv.at[i * chips]).wait()
+
+        @pl.loop(1, chips)
+        def _(j):
+            table_copy(i * chips + j, tables_ref.at[slot], slot, chip_peer(j)).start()
+
+        pass_copy(slot, tables_ref.at[slot]).start()
+
     probe_tiles = pkey_ref.shape[3]
     hi_iota = lax.broadcasted_iota(jnp.int32, (PARTS_SIZE // LANES, LANES), 0)
     lo_iota = lax.broadcasted_iota(jnp.int32, (LANES, LANES), 0)
@@ -169,11 +186,12 @@
     def _(k):
         h1_copy(k).start()
 
-    @pl.loop(1, rows * chips)
-    def _(k):
-        sr, sc = chip_source(k)
+    @pl.loop(0, rows * (chips - 1))
+    def _(k):
+        at = k // (chips - 1) * chips + lax.rem(k, chips - 1) + 1
+        sr, sc = chip_source(at)
         slot = sr * cols + sc
-        pltpu.make_async_copy(tables_ref.at[slot], tables_ref.at[slot], table_recv.at[k]).wait()
+        pltpu.make_async_copy(tables_ref.at[slot], tables_ref.at[slot], table_recv.at[at]).wait()
         pass_copy(slot, tables_ref.at[slot]).start()
 
     hist1_rest = hist1.at[pl.ds(0, cols - 1)]

time: 49.9 us -> 40 us (0.80)
  Pallas kernels: 45.2 us -> 35.3 us
    pallas_call x1, Pallas kernels: 39.1 us -> 29.1 us  [local(): pl.pallas_call(functools.partial(gather_kernel, rows, cols, local_tiles),...]
where the time goes in v3:
time: 40 us; the launch traced here: 39.7 us
  Pallas kernels  35.3 us (88%)
  local copies, waits for them, and re-layouts  3.75 us (9%)
  between operations  0.65 us (2%)
    pallas_call x1, Pallas kernels, local(): pl.pallas_call(functools.partial(gather_kernel, rows, cols, local_tiles),...  29.1 us
    pallas_call x1, Pallas kernels, local(): pl.pallas_call(join_kernel, grid=(owners,), out_shape=(jax.ShapeDtypeStru...  6.12 us
    unnamed x10, local copies, waits for them, and re-layouts  3.75 us

profile of v3, /device:TPU:0, one launch (start us, length us, event | category | flops | bytes accessed | tf_op | source)
XLA Modules:
  0.0 39.7 jit_solution(10380565178420387853)
XLA Ops:
  0.6 0.0 copy-start
  0.6 0.7 %copy-done = s32[1,1,8,8,128]{4,3,2,1,0:T(8,128)S(1)} copy-done((s32[1,1,8,8,128]{4,3,2,1,0:T(8,128)S(1)}, s32[1,1,8,8,128]{4,3,2,1,0:T(8,128)}, u32[]{:S(2)}) %copy-start) | copy-done | bytes 32792
  1.4 0.0 copy-start.1
  1.4 0.8 %copy-done.1 = s32[1,1,8,8,128]{4,3,2,1,0:T(8,128)S(1)} copy-done((s32[1,1,8,8,128]{4,3,2,1,0:T(8,128)S(1)}, s32[1,1,8,8,128]{4,3,2,1,0:T(8,128)}, u32[]{:S(2)}) %copy-start.1) | copy-done | bytes 32792
  2.1 0.0 copy-start.2
  2.2 0.9 %copy-done.2 = f32[1,2,128,128]{3,2,1,0:T(8,128)S(1)} copy-done((f32[1,2,128,128]{3,2,1,0:T(8,128)S(1)}, f32[1,2,128,128]{3,2,1,0:T(8,128)}, u32[]{:S(2)}) %copy-start.2) | copy-done | bytes 131096
  3.1 0.0 copy-start.3
  3.1 0.7 %copy-done.3 = s32[1,2,128]{2,1,0:T(2,128)S(1)} copy-done((s32[1,2,128]{2,1,0:T(2,128)S(1)}, s32[1,2,128]{2,1,0:T(2,128)}, u32[]{:S(2)}) %copy-start.3) | copy-done | bytes 1048
  3.7 0.0 copy-start.4
  3.7 0.7 %copy-done.4 = s32[1,2]{1,0:T(1,128)S(1)} copy-done((s32[1,2]{1,0:T(1,128)S(1)}, s32[1,2]{1,0:T(1,128)}, u32[]{:S(2)}) %copy-start.4) | copy-done | bytes 32
  4.4 29.1 %shard_map.76 = (f32[32,128,128]{2,1,0:T(8,128)S(1)}, f32[32,8,128]{2,1,0:T(8,128)S(1)}, f32[8,8,128]{2,1,0:T(8,128)S(1)}, f32[8,128]{1,0:T(8,128)S(1)}) custom-call(s32[1,2,128]{2,1,0:T(2,128)S(1)} %copy-done.3, s32[1,2]{1,0:T(1,128)S(1)} %copy-done.4, f32[1,2,128,128]{3,2,1,0:T(8,128)S(1)} %copy-done.2, s32[1,1,8,8,128]{4,3,2,1,0:T(8,128)S(1)} %copy-done, ...), custom_call_target="tpu_custom_call" | custom-call | tf_op jit(solution)/shard_map/pallas_call | solution.py:257
  33.5 6.1 %shard_map.77 = (f32[1,1,8,8,128,128]{5,4,3,2,1,0:T(8,128)}, f32[1,1,8,8,128]{4,3,2,1,0:T(8,128)}, f32[8,128]{1,0:T(8,128)}) custom-call(f32[4,8,128,128]{3,2,1,0:T(8,128)S(1)} %bitcast.3, f32[4,8,8,128]{3,2,1,0:T(8,128)S(1)} %bitcast.4, s32[1,1,8,8,128]{4,3,2,1,0:T(8,128)S(1)} %copy-done, s32[1,1,8,8,128]{4,3,2,1,0:T(8,128)S(1)} %copy-done.1, ...), custom_call_target="tpu_custom_call" | custom-call | tf_op jit(solution)/shard_map/pallas_call | solution.py:286
Async XLA Ops:
  0.6 0.8 %copy-start = (s32[1,1,8,8,128]{4,3,2,1,0:T(8,128)S(1)}, s32[1,1,8,8,128]{4,3,2,1,0:T(8,128)}, u32[]{:S(2)}) copy-start(s32[1,1,8,8,128]{4,3,2,1,0:T(8,128)} %pkey_ref.1) | copy-start | bytes 98308
  1.4 0.8 %copy-start.1 = (s32[1,1,8,8,128]{4,3,2,1,0:T(8,128)S(1)}, s32[1,1,8,8,128]{4,3,2,1,0:T(8,128)}, u32[]{:S(2)}) copy-start(s32[1,1,8,8,128]{4,3,2,1,0:T(8,128)} %ppart_ref.1) | copy-start | bytes 98308
  2.1 0.9 %copy-start.2 = (f32[1,2,128,128]{3,2,1,0:T(8,128)S(1)}, f32[1,2,128,128]{3,2,1,0:T(8,128)}, u32[]{:S(2)}) copy-start(f32[1,2,128,128]{3,2,1,0:T(8,128)} %pay_hbm.1) | copy-start | bytes 393220
  3.1 0.7 %copy-start.3 = (s32[1,2,128]{2,1,0:T(2,128)S(1)}, s32[1,2,128]{2,1,0:T(2,128)}, u32[]{:S(2)}) copy-start(s32[1,2,128]{2,1,0:T(2,128)} %bkey_hbm.1) | copy-start | bytes 3076
  3.7 0.7 %copy-start.4 = (s32[1,2]{1,0:T(1,128)S(1)}, s32[1,2]{1,0:T(1,128)}, u32[]{:S(2)}) copy-start(s32[1,2]{1,0:T(1,128)} %bpart_hbm.1) | copy-start | bytes 28
